TPU v7x, 512 devices: a 8x2x16 block of a 8x8x16 slice. The times are simulated.
512 devices in a mesh: groups: 2 (over y), wide: 128 (over x, z), narrow: 2 (over core).
Axes of the slice: x: 8, y: 2, z: 16, core: 2. Of those that a mesh axis runs over, the one named last changes fastest.
The devices are a block of a 8x8x16 slice.
Arguments:
- hidden_in: bfloat16 [102400, 1024], P(('groups', 'wide')), parts along dimension 0, may hold values from -6 to 6
- ffn_gain: bfloat16 [1024], replicated, may hold values from 0.5 to 1.5
- wi_gate: bfloat16 [1024, 2816], P('wide', 'narrow'), may hold values from -0.1875 to 0.1875
- wi_up: bfloat16 [1024, 2816], P('wide', 'narrow'), may hold values from -0.1875 to 0.1875
- wo_down: bfloat16 [2816, 1024], P('narrow', 'wide'), may hold values from -0.109375 to 0.109375
- final_gain: bfloat16 [1024], replicated, may hold values from 0.5 to 1.5
- key_w: bfloat16 [1024, 1024], P('wide', 'narrow'), may hold values from -0.1875 to 0.1875
- value_w: bfloat16 [1024, 1024], P('wide', 'narrow'), may hold values from -0.1875 to 0.1875
- query_w: bfloat16 [1024, 1024], P('wide', 'narrow'), may hold values from -8 to 8
- out_w: bfloat16 [1024, 1024], P('narrow', 'wide'), may hold values from -0.1875 to 0.1875
- dec_gain: bfloat16 [1024], replicated, may hold values from 0.5 to 1.5
- embed: bfloat16 [32128, 1024], P('wide'), may hold values from -6 to 6
- lengths: int32 [512], P(('groups', 'wide')), parts along dimension 0, may hold values from 40 to 200
- answer_ids: int32 [8, 32], P('groups'), parts along dimension 0, may hold values from 0 to 32127
Outputs:
- memory: bfloat16 [102400, 1024], P(('groups', 'wide')), parts along dimension 0
- decoded: bfloat16 [256, 1024], P('groups', 'narrow'), parts along dimension 0
There are 2 independent parts, one for each index of `groups`. A program takes and returns all parts, laid end to end along the dimension named above; an argument that names none is the same for every part. Nothing has to cross between parts.
All inputs are finite; a program needn't handle non-finite values.
Results may differ from a plain program's by a relative error of at most 0.0095.
The roundings to bfloat16 on the way count: a program that leaves them out, or rounds other values in their place, can miss the bound.
Values may be sent and summed in bfloat16 or wider, within the bound.
A program may use at most 64 MiB of HBM per device.

v0:
```python
import math
import jax
import jax.numpy as jnp
from jax import lax
from jax.sharding import Mesh
from jax.sharding import PartitionSpec as P

HEAD_DIM = 64
QUEST = 4
WIDE = ("wide_0", "wide_1")
GROUPS_WIDE = ("groups", "wide_0", "wide_1")
EPS = 1e-06
FLOOR = -1e30


def in_one_piece(arrays, axis, dim, along):
    ends, at = ([], 0)
    for a in arrays[:-1]:
        at += a.shape[along]
        ends.append(at)
    both = jnp.concatenate(arrays, axis=along)
    return tuple(jnp.split(lax.all_gather(both, axis, axis=dim, tiled=True), ends, axis=along))


def in_order(tiles, dim):
    tiles = jnp.moveaxis(tiles, 0, dim)
    lengths = tiles.shape
    return tiles.reshape(*lengths[:dim], lengths[dim] * lengths[dim + 1], *lengths[dim + 2 :])


def all_blocks(x, axes, turns):
    tiles = x
    for k in turns:
        tiles = lax.all_gather(tiles, axes[k])
    done = turns[::-1]
    back = [done.index(k) for k in range(len(axes))]
    tiles = tiles.transpose(*back, *range(len(axes), tiles.ndim))
    return tiles.reshape(-1, *x.shape)


def whole_of(x, axes, turns, dim):
    return in_order(all_blocks(x, axes, turns), dim)


def from_everyone(x, axis):
    copies = jnp.broadcast_to(x, (lax.axis_size(axis), *x.shape))
    return lax.all_to_all(copies, axis, split_axis=0, concat_axis=0, tiled=True)


def over_copies(x, axis):
    return from_everyone(x, axis).sum(axis=0)


def collected_together(x, axis):
    leaves = jax.tree.leaves(x)
    turns = sorted(range(len(leaves)), key=lambda k: -leaves[k].size)
    width = (1, *leaves[turns[0]].shape)[-1]
    lines = [
        jnp.pad(leaves[k].reshape(-1), (0, -leaves[k].size % width)).reshape(-1, width)
        for k in turns
    ]
    both, at, found = (lax.all_gather(jnp.concatenate(lines), axis), 0, {})
    for k, line in zip(turns, lines):
        piece = both[:, at : at + len(line)].reshape(len(both), -1)
        found[k] = piece[:, : leaves[k].size].reshape(-1, *leaves[k].shape)
        at += len(line)
    numbers = iter(range(len(leaves)))
    return jax.tree.map(lambda _: found[next(numbers)], x)


def joined_all(x, axes, combine):
    for axis in axes:
        pieces = collected_together(x, axis)
        x = jax.tree.map(lambda part: part[0], pieces)
        for k in range(1, lax.axis_size(axis)):
            x = combine(x, jax.tree.map(lambda part: part[k], pieces))
    return x


def split_up(x, dim, devices):
    lengths = x.shape
    tiles = x.reshape(*lengths[:dim], devices, lengths[dim] // devices, *lengths[dim + 1 :])
    return jnp.moveaxis(tiles, dim, 0)


def sum_at_owner(x, axis, dim):
    tiles = split_up(x, dim, lax.axis_size(axis))
    arrived = lax.all_to_all(tiles, axis, split_axis=0, concat_axis=0, tiled=True)
    return arrived.astype(jnp.float32).sum(axis=0)


def rms_scale(values, gain):
    mean_square = jnp.mean(values * values, axis=-1, keepdims=True)
    return values * lax.rsqrt(mean_square + EPS) * gain.astype(jnp.float32)


def join_partial(first, second):
    top_first, total_first, acc_first = first
    top_second, total_second, acc_second = second
    top = jnp.maximum(top_first, top_second)
    factor_first = jnp.exp(top_first - top)
    factor_second = jnp.exp(top_second - top)
    width = acc_first.shape[1] // top.shape[1]
    total = total_first * factor_first + total_second * factor_second
    acc = acc_first * jnp.repeat(factor_first, width, axis=1) + acc_second * jnp.repeat(
        factor_second, width, axis=1
    )
    return (top, total, acc)


def per_device(
    hidden_in,
    ffn_gain,
    wi_gate,
    wi_up,
    wo_down,
    final_gain,
    key_w,
    value_w,
    query_w,
    out_w,
    dec_gain,
    embed,
    lengths,
    answer_ids,
):
    rows = hidden_in.shape[0]
    resid_in = hidden_in.astype(jnp.float32)
    enc_in = rms_scale(resid_in, ffn_gain).astype(jnp.bfloat16)
    gate_full, up_full = in_one_piece((wi_gate, wi_up), WIDE, 0, 1)
    gate = jnp.dot(enc_in, gate_full, preferred_element_type=jnp.float32)
    up = jnp.dot(enc_in, up_full, preferred_element_type=jnp.float32)
    inner = (jax.nn.gelu(gate, approximate=True) * up).astype(jnp.bfloat16)
    down_full = whole_of(wo_down, WIDE, (0, 1), 1)
    partial_down = jnp.dot(inner, down_full, preferred_element_type=jnp.float32)
    resid = resid_in + over_copies(partial_down, "narrow")
    memory = rms_scale(resid, final_gain).astype(jnp.bfloat16)
    pass_dev = lengths.shape[0]
    per_question = pass_dev * lax.axis_size(WIDE) // QUEST
    question = lax.axis_index(WIDE) * pass_dev // per_question
    answers = answer_ids.shape[1]
    qrows = answer_ids.shape[0] * answers
    vocab_rows = embed.shape[0]
    local_ids = answer_ids.reshape(qrows) - lax.axis_index(WIDE) * vocab_rows
    onehot = (local_ids[:, None] == jnp.arange(vocab_rows, dtype=jnp.int32)[None, :]).astype(
        jnp.bfloat16
    )
    embedded = lax.psum(jnp.dot(onehot, embed, preferred_element_type=jnp.float32), WIDE)
    dec_in = rms_scale(embedded, dec_gain).astype(jnp.bfloat16)
    own_rows = lax.dynamic_slice_in_dim(dec_in, question * answers, answers, 0)
    proj_cols = key_w.shape[1]
    key_full, value_full, query_full = in_one_piece((key_w, value_w, query_w), WIDE, 0, 1)
    keys_sum = jnp.dot(memory, key_full, preferred_element_type=jnp.float32)
    values_sum = jnp.dot(memory, value_full, preferred_element_type=jnp.float32)
    query_sum = jnp.dot(own_rows, query_full, preferred_element_type=jnp.float32)
    keys = keys_sum.astype(jnp.bfloat16)
    values = values_sum.astype(jnp.bfloat16)
    query = query_sum.astype(jnp.bfloat16)
    heads_local = proj_cols // HEAD_DIM
    query_three = query.reshape(answers, heads_local, HEAD_DIM)
    keys_three = keys.reshape(rows, heads_local, HEAD_DIM)
    values_three = values.reshape(rows, heads_local, HEAD_DIM).astype(jnp.float32)
    scores = jnp.einsum(
        "ahd,khd->ahk", query_three, keys_three, preferred_element_type=jnp.float32
    ) * (1.0 / math.sqrt(HEAD_DIM))
    passage_len = rows // pass_dev
    live = (jnp.arange(passage_len, dtype=jnp.int32)[None, :] < lengths[:, None]).reshape(rows)
    scores = jnp.where(live[None, None, :], scores, FLOOR)
    top = jnp.max(scores, axis=2)
    weights = jnp.exp(scores - top[:, :, None])
    total = jnp.sum(weights, axis=2)
    acc = jnp.einsum("ahk,khd->ahd", weights, values_three).reshape(answers, proj_cols)
    start_row = question * answers
    top_all = lax.dynamic_update_slice_in_dim(
        jnp.full((qrows, heads_local), FLOOR, jnp.float32), top, start_row, 0
    )
    total_all = lax.dynamic_update_slice_in_dim(
        jnp.zeros((qrows, heads_local), jnp.float32), total, start_row, 0
    )
    acc_all = lax.dynamic_update_slice_in_dim(
        jnp.zeros((qrows, proj_cols), jnp.float32), acc, start_row, 0
    )
    top_all, total_all, acc_all = joined_all((top_all, total_all, acc_all), WIDE, join_partial)
    attended = (acc_all / jnp.repeat(total_all, HEAD_DIM, axis=1)).astype(jnp.bfloat16)
    out_full = whole_of(out_w, WIDE, (0, 1), 1)
    partial_out = jnp.dot(attended, out_full, preferred_element_type=jnp.float32)
    share_out = sum_at_owner(partial_out.astype(jnp.bfloat16), "narrow", 1)
    out_half = share_out.shape[1]
    embedded_half = lax.dynamic_slice_in_dim(
        embedded, lax.axis_index("narrow") * out_half, out_half, 1
    )
    decoded = (embedded_half + share_out).astype(jnp.bfloat16)
    return (memory, decoded)


def solution(mesh):
    torus = Mesh(
        mesh.devices.reshape(mesh.shape["groups"], 8, 16, mesh.shape["narrow"]),
        ("groups", "wide_0", "wide_1", "narrow"),
    )
    return jax.shard_map(
        per_device,
        mesh=torus,
        in_specs=(
            P(GROUPS_WIDE, None),
            P(),
            P(WIDE, "narrow"),
            P(WIDE, "narrow"),
            P("narrow", WIDE),
            P(),
            P(WIDE, "narrow"),
            P(WIDE, "narrow"),
            P(WIDE, "narrow"),
            P("narrow", WIDE),
            P(),
            P(WIDE, None),
            P(GROUPS_WIDE),
            P("groups", None),
        ),
        out_specs=(P(GROUPS_WIDE, None), P("groups", "narrow")),
        check_vma=False,
    )
```

profile of v0, /device:TPU:65, one launch (start us, length us, event | category | flops | bytes accessed | tf_op | source)
XLA Modules:
  0.0 730.1 jit_solution(12528337579370721748)
XLA Ops:
  9.1 1.1 fusion.40
  10.3 23.2 %all-gather = bf16[11264,8]{0,1:T(8,128)(2,1)} all-gather(bf16[1408,8]{0,1:T(8,128)(2,1)} %param.18), channel_id=2, replica_groups=mesh['groups'=2,'wide_0'=8,'wide_1'=16,'narrow'=2] {'wide_0'}, dimensions={0}, use_global_device_ids=true | all-gather | bytes 202752 | tf_op jit(solution)/shard_map/all_gather | solution.py:34
  33.6 1.3 pad_maximum_fusion.1
  35.1 1.4 pad_maximum_fusion
  38.4 277.3 %all-reduce.2.cloned.1.call-done = f32[128,1024]{1,0:T(8,128)} async-done(((f32[128,1024]{1,0:T(8,128)}), f32[128,1024]{1,0:T(8,128)}) %all-reduce.2.cloned.1.call-update) | async-done | bytes 524304 | tf_op jit(solution)/shard_map/psum | solution.py:148
  315.7 1.2 multiply_reduce_fusion.1
  317.0 3.8 copy.413
  320.8 1.5 convolution_convert_fusion.3
  323.1 111.4 %all-gather.15.cloned.1.call-done = bf16[1024,2816]{1,0:T(8,128)(2,1)} async-done(((bf16[8,2816]{1,0:T(8,128)(2,1)}), bf16[1024,2816]{1,0:T(8,128)(2,1)}) %all-gather.15.cloned.1.call-update) | async-done | bytes 5767184 | tf_op jit(solution)/shard_map/all_gather | solution.py:22
  434.4 4.9 fusion.12
  439.4 6.1 fusion.24
  445.9 15.5 %all_to_all.10 = f32[2,400,1024]{2,1,0:T(8,128)} all-to-all(f32[2,400,1024]{2,1,0:T(8,128)S(1)} %broadcast_in_dim.170), channel_id=1, replica_groups=mesh['groups'=2,'wide_0'=8,'wide_1'=16,'narrow'=2] {'narrow'}, dimensions={0} | all-to-all | bytes 6553600 | tf_op jit(solution)/shard_map/all_to_all | solution.py:47
  461.4 2.4 reduce_sum.55
  464.4 0.9 copy-done.3
  465.3 1.8 convolution_convert_fusion
  468.3 1.8 convolution_convert_fusion.1
  471.7 21.1 %all-gather.4 = bf16[4096,8]{0,1:T(8,128)(2,1)} all-gather(bf16[512,8]{0,1:T(8,128)(2,1)S(1)} %copy-done.8), channel_id=6, replica_groups=mesh['groups'=2,'wide_0'=8,'wide_1'=16,'narrow'=2] {'wide_0'}, dimensions={0}, use_global_device_ids=true | all-gather | bytes 73728 | tf_op jit(solution)/shard_map/all_gather | solution.py:34
  493.2 16.7 %all-gather.23.cloned.1.call-done = f32[8,132,512]{2,1,0:T(8,128)} async-done(((f32[1,132,512]{2,1,0:T(8,128)}), f32[8,132,512]{2,1,0:T(8,128)}) %all-gather.23.cloned.1.call-update) | async-done | bytes 2162704 | tf_op jit(solution)/shard_map/all_gather | solution.py:62
  509.8 1.0 fusion.51
  511.2 2.6 fusion.96
  514.4 1.1 copy.515
  515.5 1.8 copy.514
  517.3 0.8 copy.513
  518.1 0.8 fusion.95
  520.4 1.2 fusion.27
  521.7 0.9 copy.446
  522.7 54.6 %all-gather.21.cloned.1.call-done = bf16[128,512,8]{1,2,0:T(8,128)(2,1)} async-done(((bf16[8,512,8]{1,2,0:T(8,128)(2,1)}), bf16[128,512,8]{1,2,0:T(8,128)(2,1)}) %all-gather.21.cloned.1.call-update) | async-done | bytes 1048592 | tf_op jit(solution)/shard_map/all_gather | solution.py:34
  577.2 1.3 copy.511
  578.6 79.3 %all-gather.25.cloned.1.call-done = f32[16,132,512]{2,1,0:T(8,128)} async-done(((f32[1,132,512]{2,1,0:T(8,128)}), f32[16,132,512]{2,1,0:T(8,128)}) %all-gather.25.cloned.1.call-update) | async-done | bytes 4325392 | tf_op jit(solution)/shard_map/all_gather | solution.py:62
  657.8 3.8 fusion.94
  662.2 1.1 copy.532
  663.3 1.8 copy.531
  665.1 1.8 copy.530
  666.9 1.8 copy.529
  668.7 1.8 copy.528
  670.5 1.8 copy.527
  672.3 1.8 copy.526
  674.1 1.8 copy.525
  675.8 1.8 copy.524
  677.6 1.8 copy.523
  679.4 1.8 copy.522
  681.2 1.8 copy.521
  683.0 1.5 fusion.93
  685.5 1.6 fusion.92
  699.5 0.8 squeeze.274
  705.2 1.0 multiply_add_fusion
  706.2 2.6 divide_convert_fusion
  709.3 12.7 %all_to_all.11 = bf16[2,128,512]{2,1,0:T(8,128)(2,1)S(1)} all-to-all(bf16[2,128,512]{2,1,0:T(8,128)(2,1)S(1)} %bitcast.360), channel_id=1, replica_groups=mesh['groups'=2,'wide_0'=8,'wide_1'=16,'narrow'=2] {'narrow'}, dimensions={0} | all-to-all | bytes 524288 | tf_op jit(solution)/shard_map/all_to_all | solution.py:88
  (170 shorter events, 30.3 us)
Async XLA Ops:
  8.0 1.0 copy-start
  8.1 30.0 %copy-start.9 = (bf16[1024]{0:T(1024)(128)(2,1)S(1)}, bf16[1024]{0:T(1024)(128)(2,1)}, u32[]{:S(2)}) copy-start(bf16[1024]{0:T(1024)(128)(2,1)} %param.24) | copy-start | bytes 6148
  8.1 30.0 %copy-start.10 = (s32[2]{0:T(128)S(1)}, s32[2]{0:T(128)}, u32[]{:S(2)}) copy-start(s32[2]{0:T(128)} %param.26) | copy-start | bytes 28
  8.1 30.1 %copy-start.1 = (bf16[400,1024]{1,0:T(8,128)(2,1)S(1)}, bf16[400,1024]{1,0:T(8,128)(2,1)}, u32[]{:S(2)}) copy-start(bf16[400,1024]{1,0:T(8,128)(2,1)} %param.14) | copy-start | bytes 2457604
  8.1 307.7 %all-reduce.2.cloned.1.call-start = ((), (), s32[]{:S(2)}) async-start(), calls=%async_computation.3 | async-start | bytes 1048576 | tf_op jit(solution)/shard_map/psum | solution.py:148
  10.2 306.8 %all-gather.19.cloned.1.call-start = ((), (), s32[]{:S(2)}) async-start(), calls=%async_computation.5 | async-start | bytes 3063808 | tf_op jit(solution)/shard_map/all_gather | solution.py:34
  33.6 287.2 %all-gather.17.cloned.1.call-start = ((), (), s32[]{:S(2)}) async-start(), calls=%async_computation.4 | async-start | bytes 3170304 | tf_op jit(solution)/shard_map/all_gather | solution.py:22
  35.0 399.4 %all-gather.15.cloned.1.call-start = ((), (), s32[]{:S(2)}) async-start(), calls=%async_computation.2 | async-start | bytes 5812224 | tf_op jit(solution)/shard_map/all_gather | solution.py:22
  36.6 473.3 %all-gather.23.cloned.1.call-start = ((), (), s32[]{:S(2)}) async-start(), calls=%async_computation.7 | async-start | bytes 2506752 | tf_op jit(solution)/shard_map/all_gather | solution.py:62
  317.0 3.8 copy-start.2
  464.4 0.9 copy-start.3
  465.2 2.1 copy-start.5
  467.1 1.1 copy-start.4
  470.1 1.6 copy-start.8
  471.6 105.6 %all-gather.21.cloned.1.call-start = ((), (), s32[]{:S(2)}) async-start(), calls=%async_computation.6 | async-start | bytes 1114112 | tf_op jit(solution)/shard_map/all_gather | solution.py:34
  492.9 164.9 %all-gather.25.cloned.1.call-start = ((), (), s32[]{:S(2)}) async-start(), calls=%async_computation.8 | async-start | bytes 4734976 | tf_op jit(solution)/shard_map/all_gather | solution.py:62
  691.4 10.7 %copy-start.6 = (f32[1,2,512]{2,1,0:T(2,128)S(1)}, f32[1,2,512]{2,1,0:T(2,128)}, u32[]{:S(2)}) copy-start(f32[1,2,512]{2,1,0:T(2,128)} %get-tuple-element.67) | copy-start | bytes 12292
  692.2 9.8 %copy-start.7 = (f32[1,2,512]{2,1,0:T(2,128)S(1)}, f32[1,2,512]{2,1,0:T(2,128)}, u32[]{:S(2)}) copy-start(f32[1,2,512]{2,1,0:T(2,128)} %get-tuple-element.76) | copy-start | bytes 12292
Sparse Core Ops, SparseCore 0:
  13.0 302.6 all-reduce.1
  471.8 38.0 all-gather.22
  511.9 65.2 all-gather.20
  579.2 78.5 all-gather.24
Sparse Core Ops, SparseCore 1:
  33.7 106.3 all-gather.18
  143.5 142.1 all-gather.16
  288.5 145.9 all-gather.14
where the time goes:
time: 732 us; the launch traced here: 730 us
  waiting for transfers between devices  540 us (74%)
  blocking collectives  72.5 us (10%)
  local copies, waits for them, and re-layouts  65.7 us (9%)
  matrix products  18.4 us (3%)
  other arithmetic  17 us (2%)
  between operations  16.3 us (2%)
    psum x1, waiting for transfers between devices, per_device(): lax.psum(jnp.dot(onehot, embed, preferred_element_type=jnp.float32), WIDE)  277 us
    all_gather x2, waiting for transfers between devices, in_one_piece(): lax.all_gather(both, axis, axis=dim, tiled=True)  111 us
    all_gather x2, waiting for transfers between devices, collected_together(): both, at, found = (lax.all_gather(jnp.concatenate(lines), axis), 0, {})  95.9 us
    all_gather x2, waiting for transfers between devices, all_blocks(): tiles = lax.all_gather(tiles, axes[k])  54.6 us
    all_gather x2, blocking collectives, all_blocks(): tiles = lax.all_gather(tiles, axes[k])  44.4 us
    unnamed x47, local copies, waits for them, and re-layouts  27.5 us
    squeeze x74, local copies, waits for them, and re-layouts, joined_all(): x = combine(x, jax.tree.map(lambda part: part[k], pieces))  18.4 us
    all_to_all x1, blocking collectives, from_everyone(): return lax.all_to_all(copies, axis, split_axis=0, concat_axis=0, tiled=True)  15.5 us
  transfers between devices with their start and end apart: 7, of which 5 were waited for; matrix products, arithmetic and copies ran while one was open for 4% of the time, Pallas kernels for 0%

commit v1 on v0

--- a/solution.py
+++ b/solution.py
@@ -145,7 +145,9 @@
     onehot = (local_ids[:, None] == jnp.arange(vocab_rows, dtype=jnp.int32)[None, :]).astype(
         jnp.bfloat16
     )
-    embedded = lax.psum(jnp.dot(onehot, embed, preferred_element_type=jnp.float32), WIDE)
+    embedded = lax.psum(
+        lax.psum(jnp.dot(onehot, embed, preferred_element_type=jnp.float32), "wide_0"), "wide_1"
+    )
     dec_in = rms_scale(embedded, dec_gain).astype(jnp.bfloat16)
     own_rows = lax.dynamic_slice_in_dim(dec_in, question * answers, answers, 0)
     proj_cols = key_w.shape[1]

time: 732 us -> 932 us (1.27)
  waiting for transfers between devices: 540 us -> 746 us
    all_gather x2, waiting for transfers between devices: 111 us -> 288 us  [in_one_piece(): lax.all_gather(both, axis, axis=dim, tiled=True)]
    all_gather x2, waiting for transfers between devices: 54.6 us -> 129 us  [all_blocks(): tiles = lax.all_gather(tiles, axes[k])]
    psum x1 -> x2, waiting for transfers between devices: 277 us -> 233 us  [the longest x1 118 us: per_device(): lax.psum(jnp.dot(onehot, embed, preferred_element_type=jnp.float32), 'wid...]
    unnamed x47 -> x61, local copies, waits for them, and re-layouts: 27.5 us -> 27.4 us
  transfers between devices with their start and end apart: 7 -> 8, of which waited for: 5 -> 8; matrix products, arithmetic and copies ran while one was open for 4% -> 2% of each run, Pallas kernels for 0% -> 0%
where the time goes in v1:
time: 932 us; the launch traced here: 931 us
  waiting for transfers between devices  746 us (80%)
  blocking collectives  70.7 us (8%)
  local copies, waits for them, and re-layouts  65.5 us (7%)
  matrix products  18.4 us (2%)
  between operations  15.1 us (2%)
  other arithmetic  14.3 us (2%)
    all_gather x2, waiting for transfers between devices, in_one_piece(): lax.all_gather(both, axis, axis=dim, tiled=True)  288 us
    all_gather x2, waiting for transfers between devices, all_blocks(): tiles = lax.all_gather(tiles, axes[k])  129 us
    psum x1, waiting for transfers between devices, per_device(): lax.psum(jnp.dot(onehot, embed, preferred_element_type=jnp.float32), 'wid...  118 us
    psum x1, waiting for transfers between devices, per_device(): lax.psum(lax.psum(jnp.dot(onehot, embed, preferred_element_type=jnp.float...  115 us
    all_gather x2, waiting for transfers between devices, collected_together(): both, at, found = (lax.all_gather(jnp.concatenate(lines), axis), 0, {})  95.5 us
    all_gather x2, blocking collectives, all_blocks(): tiles = lax.all_gather(tiles, axes[k])  42.2 us
    unnamed x61, local copies, waits for them, and re-layouts  27.4 us
  transfers between devices with their start and end apart: 8, of which 8 were waited for; matrix products, arithmetic and copies ran while one was open for 2% of the time, Pallas kernels for 0%

profile of v1, /device:TPU:65, one launch (start us, length us, event | category | flops | bytes accessed | tf_op | source)
XLA Modules:
  0.0 930.8 jit_solution(6448531791263369525)
XLA Ops:
  7.4 0.9 broadcast_subtract_fusion
  8.3 1.1 fusion.40
  9.5 117.7 %all-reduce.3.cloned.1.call-done = f32[128,1024]{1,0:T(8,128)} async-done(((f32[128,1024]{1,0:T(8,128)}), f32[128,1024]{1,0:T(8,128)}) %all-reduce.3.cloned.1.call-update) | async-done | bytes 524304 | tf_op jit(solution)/shard_map/psum | solution.py:149
  127.4 21.0 %all-gather = bf16[11264,8]{0,1:T(8,128)(2,1)} all-gather(bf16[1408,8]{0,1:T(8,128)(2,1)} %param.18), channel_id=2, replica_groups=mesh['groups'=2,'wide_0'=8,'wide_1'=16,'narrow'=2] {'wide_0'}, dimensions={0}, use_global_device_ids=true | all-gather | bytes 202752 | tf_op jit(solution)/shard_map/all_gather | solution.py:34
  150.6 114.9 %all-reduce.5.cloned.1.call-done = f32[128,1024]{1,0:T(8,128)} async-done(((f32[128,1024]{1,0:T(8,128)}), f32[128,1024]{1,0:T(8,128)}) %all-reduce.5.cloned.1.call-update) | async-done | bytes 524304 | tf_op jit(solution)/shard_map/psum | solution.py:148
  265.4 1.2 multiply_reduce_fusion.1
  266.7 74.6 %all-gather.19.cloned.1.call-done = bf16[128,1408,8]{1,2,0:T(8,128)(2,1)} async-done(((bf16[8,1408,8]{1,2,0:T(8,128)(2,1)}), bf16[128,1408,8]{1,2,0:T(8,128)(2,1)}) %all-gather.19.cloned.1.call-update) | async-done | bytes 2883600 | tf_op jit(solution)/shard_map/all_gather | solution.py:34
  341.3 3.7 copy.413
  345.0 141.3 %all-gather.17.cloned.1.call-done = bf16[1024,1536]{1,0:T(8,128)(2,1)} async-done(((bf16[8,1536]{1,0:T(8,128)(2,1)}), bf16[1024,1536]{1,0:T(8,128)(2,1)}) %all-gather.17.cloned.1.call-update) | async-done | bytes 3145744 | tf_op jit(solution)/shard_map/all_gather | solution.py:22
  486.3 1.5 convolution_convert_fusion.3
  488.6 147.0 %all-gather.15.cloned.1.call-done = bf16[1024,2816]{1,0:T(8,128)(2,1)} async-done(((bf16[8,2816]{1,0:T(8,128)(2,1)}), bf16[1024,2816]{1,0:T(8,128)(2,1)}) %all-gather.15.cloned.1.call-update) | async-done | bytes 5767184 | tf_op jit(solution)/shard_map/all_gather | solution.py:22
  635.6 4.9 fusion.12
  640.6 6.1 fusion.24
  647.1 15.8 %all_to_all.10 = f32[2,400,1024]{2,1,0:T(8,128)} all-to-all(f32[2,400,1024]{2,1,0:T(8,128)S(1)} %broadcast_in_dim.170), channel_id=1, replica_groups=mesh['groups'=2,'wide_0'=8,'wide_1'=16,'narrow'=2] {'narrow'}, dimensions={0} | all-to-all | bytes 6553600 | tf_op jit(solution)/shard_map/all_to_all | solution.py:47
  662.9 2.4 reduce_sum.55
  665.9 0.9 copy-done.3
  666.8 1.9 convolution_convert_fusion
  669.8 1.8 convolution_convert_fusion.1
  673.3 21.2 %all-gather.4 = bf16[4096,8]{0,1:T(8,128)(2,1)} all-gather(bf16[512,8]{0,1:T(8,128)(2,1)S(1)} %copy-done.10), channel_id=6, replica_groups=mesh['groups'=2,'wide_0'=8,'wide_1'=16,'narrow'=2] {'wide_0'}, dimensions={0}, use_global_device_ids=true | all-gather | bytes 73728 | tf_op jit(solution)/shard_map/all_gather | solution.py:34
  694.8 16.1 %all-gather.23.cloned.1.call-done = f32[8,132,512]{2,1,0:T(8,128)} async-done(((f32[1,132,512]{2,1,0:T(8,128)}), f32[8,132,512]{2,1,0:T(8,128)}) %all-gather.23.cloned.1.call-update) | async-done | bytes 2162704 | tf_op jit(solution)/shard_map/all_gather | solution.py:62
  710.9 1.0 fusion.51
  712.2 2.6 fusion.96
  715.4 1.1 copy.515
  716.5 1.8 copy.514
  719.2 0.8 fusion.95
  721.4 1.2 fusion.27
  722.8 0.9 copy.446
  723.8 54.7 %all-gather.21.cloned.1.call-done = bf16[128,512,8]{1,2,0:T(8,128)(2,1)} async-done(((bf16[8,512,8]{1,2,0:T(8,128)(2,1)}), bf16[128,512,8]{1,2,0:T(8,128)(2,1)}) %all-gather.21.cloned.1.call-update) | async-done | bytes 1048592 | tf_op jit(solution)/shard_map/all_gather | solution.py:34
  778.4 1.3 copy.511
  779.8 79.4 %all-gather.25.cloned.1.call-done = f32[16,132,512]{2,1,0:T(8,128)} async-done(((f32[1,132,512]{2,1,0:T(8,128)}), f32[16,132,512]{2,1,0:T(8,128)}) %all-gather.25.cloned.1.call-update) | async-done | bytes 4325392 | tf_op jit(solution)/shard_map/all_gather | solution.py:62
  859.2 3.8 fusion.94
  863.5 1.1 copy.532
  864.6 1.8 copy.531
  866.4 1.8 copy.530
  868.2 1.8 copy.529
  870.0 1.8 copy.528
  871.8 1.8 copy.527
  873.6 1.8 copy.526
  875.3 1.8 copy.525
  877.1 1.8 copy.524
  878.9 1.8 copy.523
  880.7 1.8 copy.522
  882.5 1.8 copy.521
  884.3 1.5 fusion.93
  886.7 1.6 fusion.92
  906.5 1.0 multiply_add_fusion
  907.5 2.6 divide_convert_fusion
  910.6 12.7 %all_to_all.11 = bf16[2,128,512]{2,1,0:T(8,128)(2,1)S(1)} all-to-all(bf16[2,128,512]{2,1,0:T(8,128)(2,1)S(1)} %bitcast.360), channel_id=1, replica_groups=mesh['groups'=2,'wide_0'=8,'wide_1'=16,'narrow'=2] {'narrow'}, dimensions={0} | all-to-all | bytes 524288 | tf_op jit(solution)/shard_map/all_to_all | solution.py:88
  (187 shorter events, 31.1 us)
Async XLA Ops:
  7.2 1.2 copy-start
  7.2 141.3 %copy-start.11 = (bf16[8,512]{1,0:T(8,128)(2,1)S(1)}, bf16[8,512]{1,0:T(8,128)(2,1)}, u32[]{:S(2)}) copy-start(bf16[8,512]{1,0:T(8,128)(2,1)} %param.22) | copy-start | bytes 24580
  7.2 141.3 %copy-start.12 = (bf16[8,512]{1,0:T(8,128)(2,1)S(1)}, bf16[8,512]{1,0:T(8,128)(2,1)}, u32[]{:S(2)}) copy-start(bf16[8,512]{1,0:T(8,128)(2,1)} %param.21) | copy-start | bytes 24580
  7.2 141.3 %copy-start.13 = (bf16[8,512]{1,0:T(8,128)(2,1)S(1)}, bf16[8,512]{1,0:T(8,128)(2,1)}, u32[]{:S(2)}) copy-start(bf16[8,512]{1,0:T(8,128)(2,1)} %param.20) | copy-start | bytes 24580
  7.2 142.0 %copy-start.6 = (bf16[8,1408]{1,0:T(8,128)(2,1)S(1)}, bf16[8,1408]{1,0:T(8,128)(2,1)}, u32[]{:S(2)}) copy-start(bf16[8,1408]{1,0:T(8,128)(2,1)} %param.17) | copy-start | bytes 67588
  7.2 142.0 %copy-start.7 = (bf16[8,1408]{1,0:T(8,128)(2,1)S(1)}, bf16[8,1408]{1,0:T(8,128)(2,1)}, u32[]{:S(2)}) copy-start(bf16[8,1408]{1,0:T(8,128)(2,1)} %param.16) | copy-start | bytes 67588
  7.2 142.8 %copy-start.14 = (bf16[1024]{0:T(1024)(128)(2,1)S(1)}, bf16[1024]{0:T(1024)(128)(2,1)}, u32[]{:S(2)}) copy-start(bf16[1024]{0:T(1024)(128)(2,1)} %param.15) | copy-start | bytes 6148
  7.3 142.8 %copy-start.15 = (bf16[1024]{0:T(1024)(128)(2,1)S(1)}, bf16[1024]{0:T(1024)(128)(2,1)}, u32[]{:S(2)}) copy-start(bf16[1024]{0:T(1024)(128)(2,1)} %param.19) | copy-start | bytes 6148
  7.3 142.9 %copy-start.16 = (bf16[1024]{0:T(1024)(128)(2,1)S(1)}, bf16[1024]{0:T(1024)(128)(2,1)}, u32[]{:S(2)}) copy-start(bf16[1024]{0:T(1024)(128)(2,1)} %param.24) | copy-start | bytes 6148
  7.3 142.9 %copy-start.17 = (s32[2]{0:T(128)S(1)}, s32[2]{0:T(128)}, u32[]{:S(2)}) copy-start(s32[2]{0:T(128)} %param.26) | copy-start | bytes 28
  7.3 143.0 %copy-start.1 = (bf16[400,1024]{1,0:T(8,128)(2,1)S(1)}, bf16[400,1024]{1,0:T(8,128)(2,1)}, u32[]{:S(2)}) copy-start(bf16[400,1024]{1,0:T(8,128)(2,1)} %param.14) | copy-start | bytes 2457604
  7.3 120.0 %all-reduce.3.cloned.1.call-start = ((), (), s32[]{:S(2)}) async-start(), calls=%async_computation.3 | async-start | bytes 1048576 | tf_op jit(solution)/shard_map/psum | solution.py:149
  9.5 256.0 %all-reduce.5.cloned.1.call-start = ((), (), s32[]{:S(2)}) async-start(), calls=%async_computation.4 | async-start | bytes 1048576 | tf_op jit(solution)/shard_map/psum | solution.py:148
  127.3 214.0 %all-gather.19.cloned.1.call-start = ((), (), s32[]{:S(2)}) async-start(), calls=%async_computation.6 | async-start | bytes 3063808 | tf_op jit(solution)/shard_map/all_gather | solution.py:34
  148.4 337.9 %all-gather.17.cloned.1.call-start = ((), (), s32[]{:S(2)}) async-start(), calls=%async_computation.5 | async-start | bytes 3170304 | tf_op jit(solution)/shard_map/all_gather | solution.py:22
  149.2 486.4 %all-gather.15.cloned.1.call-start = ((), (), s32[]{:S(2)}) async-start(), calls=%async_computation.2 | async-start | bytes 5812224 | tf_op jit(solution)/shard_map/all_gather | solution.py:22
  150.0 560.9 %all-gather.23.cloned.1.call-start = ((), (), s32[]{:S(2)}) async-start(), calls=%async_computation.8 | async-start | bytes 2506752 | tf_op jit(solution)/shard_map/all_gather | solution.py:62
  341.3 145.0 %copy-start.2 = (f32[128,1024]{1,0:T(8,128)S(1)}, f32[128,1024]{1,0:T(8,128)}, u32[]{:S(2)}) copy-start(f32[128,1024]{1,0:T(8,128)} %all-reduce.5.cloned.1.call-done) | copy-start | bytes 1572868
  665.9 0.9 copy-start.3
  666.8 2.1 copy-start.5
  668.6 1.1 copy-start.4
  671.6 1.6 copy-start.10
  673.2 105.3 %all-gather.21.cloned.1.call-start = ((), (), s32[]{:S(2)}) async-start(), calls=%async_computation.7 | async-start | bytes 1114112 | tf_op jit(solution)/shard_map/all_gather | solution.py:34
  694.5 164.6 %all-gather.25.cloned.1.call-start = ((), (), s32[]{:S(2)}) async-start(), calls=%async_computation.9 | async-start | bytes 4734976 | tf_op jit(solution)/shard_map/all_gather | solution.py:62
  892.7 10.7 %copy-start.8 = (f32[1,2,512]{2,1,0:T(2,128)S(1)}, f32[1,2,512]{2,1,0:T(2,128)}, u32[]{:S(2)}) copy-start(f32[1,2,512]{2,1,0:T(2,128)} %get-tuple-element.67) | copy-start | bytes 12292
  893.5 9.8 %copy-start.9 = (f32[1,2,512]{2,1,0:T(2,128)S(1)}, f32[1,2,512]{2,1,0:T(2,128)}, u32[]{:S(2)}) copy-start(f32[1,2,512]{2,1,0:T(2,128)} %get-tuple-element.76) | copy-start | bytes 12292
Sparse Core Ops, SparseCore 0:
  11.1 116.1 all-reduce.2
  129.6 135.7 all-reduce.4
  267.5 73.7 all-gather.18
  344.7 141.5 all-gather.16
  489.7 145.8 all-gather.14
  673.3 37.5 all-gather.22
  713.0 65.3 all-gather.20
  780.5 78.5 all-gather.24
